TPU v7x, 32 devices: a whole 2x2x4 slice. The times are simulated.
32 devices in a mesh: dp: 8 (over z, x), tensor: 4 (over y, core).
Axes of the slice: x: 2, y: 2, z: 4, core: 2. Of those that a mesh axis runs over, the one named last changes fastest.
Arguments:
- tokens: bfloat16 [8, 256, 4096], P('dp', 'tensor'), may hold values from -6 to 6
- gain: bfloat16 [4096], replicated, may hold values from 0.5 to 1.5
- wq: bfloat16 [4096, 4096], P(None, 'tensor'), may hold values from -0.09375 to 0.09375
- bq: bfloat16 [4096], P('tensor'), may hold values from -5 to 5
- wkv: bfloat16 [4096, 1024], P(None, 'tensor'), may hold values from -0.09375 to 0.09375
- bkv: bfloat16 [1024], P('tensor'), may hold values from -5 to 5
- wo: bfloat16 [4096, 4096], P('tensor'), may hold values from -0.375 to 0.375
- check_weights: float32 [8, 256], P('dp'), may hold values from -12 to 12
Outputs:
- attended: bfloat16 [8, 256, 4096], P('dp', 'tensor')
- checksum: float32 [4096], replicated
All inputs are finite; a program needn't handle non-finite values.
Results may differ from a plain program's by a relative error of at most 0.018.
Values may be sent and summed in bfloat16 or wider, within the bound.
A program may use at most 64 MiB of HBM per device.

v0:
```python
import jax
import jax.numpy as jnp
from jax import lax
from jax.sharding import PartitionSpec as P

HEADS = 32
KV = 4
HD = 128
EPS = 1e-06
THETA = 1000000.0


def rope(values, head_size):
    rows = values.shape[0]
    half = head_size // 2
    inverse = THETA ** (-(jnp.arange(half, dtype=jnp.float32) * 2.0 / head_size))
    angles = jnp.arange(rows, dtype=jnp.float32)[:, None] * inverse[None, :]
    cosine = jnp.cos(angles)[:, None, :]
    sine = jnp.sin(angles)[:, None, :]
    shaped = values.reshape(rows, -1, head_size)
    first = shaped[..., :half]
    second = shaped[..., half:]
    turned = jnp.concatenate(
        [first * cosine - second * sine, second * cosine + first * sine], axis=-1
    )
    return turned.reshape(rows, -1)


def local(tokens, gain, wq, bq, wkv, bkv, wo, check_weights):
    states = tokens[0].astype(jnp.float32)
    normed = (
        states
        * lax.rsqrt(jnp.mean(states * states, axis=-1, keepdims=True) + EPS)
        * gain.astype(jnp.float32)
    ).astype(jnp.bfloat16)
    position = lax.axis_index("tensor")
    head_dev = wq.shape[1] // HD
    query_cols = head_dev * HD
    shared = position * head_dev // (HEADS // KV)
    joined_w = jnp.concatenate([wq, wkv], axis=1)
    joined_b = jnp.concatenate([bq, bkv], axis=0).astype(jnp.float32)
    projected = (
        jnp.dot(
            lax.all_gather(normed, "tensor", axis=0, tiled=True),
            joined_w,
            preferred_element_type=jnp.float32,
        )
        + joined_b[None, :]
    )
    seq_rows = projected.shape[0]
    query = rope(projected[:, :query_cols], HD).astype(jnp.bfloat16)
    kv_local = projected[:, query_cols:].astype(jnp.bfloat16)
    kv_whole = lax.all_gather(kv_local, "tensor", axis=1, tiled=True)
    key_part = lax.dynamic_slice_in_dim(kv_whole, shared * HD, HD, 1)
    values = lax.dynamic_slice_in_dim(kv_whole, KV * HD + shared * HD, HD, 1)
    keys = rope(key_part.astype(jnp.float32), HD).astype(jnp.bfloat16)
    scale = HD ** (-0.5)
    block = min(512, seq_rows)
    query_heads = query.reshape(seq_rows, head_dev, HD)
    pieces = []
    for number in range(seq_rows // block):
        stop = (number + 1) * block
        query_block = query_heads[number * block : stop]
        scores = (
            jnp.einsum("qhd,kd->hqk", query_block, keys[:stop], preferred_element_type=jnp.float32)
            * scale
        )
        allowed = jnp.arange(block)[:, None] + number * block >= jnp.arange(stop)[None, :]
        scores = jnp.where(allowed[None, :, :], scores, -1e30)
        probs = jax.nn.softmax(scores, axis=-1).astype(jnp.bfloat16)
        mixed = jnp.einsum(
            "hqk,kd->qhd", probs, values[:stop], preferred_element_type=jnp.float32
        ).astype(jnp.bfloat16)
        pieces.append(mixed.reshape(block, query_cols))
    context = jnp.concatenate(pieces, axis=0)
    summed = lax.psum_scatter(
        jnp.dot(context, wo, preferred_element_type=jnp.float32).astype(jnp.bfloat16),
        "tensor",
        scatter_dimension=0,
        tiled=True,
    )
    attended = summed[None, :, :]
    summary = jnp.dot(
        check_weights[0], context.astype(jnp.float32), precision=lax.Precision.HIGHEST
    )
    term = jnp.dot(summary, wo.astype(jnp.float32), precision=lax.Precision.HIGHEST)
    total = lax.psum(term, ("dp", "tensor"))
    checksum = total / jnp.sqrt(jnp.float32(seq_rows * lax.axis_size("dp")))
    return (attended, checksum)


def solution(mesh):
    placed = (
        P("dp", "tensor", None),
        P(),
        P(None, "tensor"),
        P("tensor"),
        P(None, "tensor"),
        P("tensor"),
        P("tensor", None),
        P("dp", None),
    )
    return jax.shard_map(
        local, mesh=mesh, in_specs=placed, out_specs=(P("dp", "tensor", None), P()), check_vma=False
    )
```

profile of v0, /device:TPU:0, one launch (start us, length us, event | category | flops | bytes accessed | tf_op | source)
XLA Modules:
  0.0 118.1 jit_solution(9520385289400516932)
XLA Ops:
  7.2 0.0 copy-start
  7.2 0.0 copy-start.1
  7.2 0.0 copy-start.2
  7.2 0.0 copy-start.3
  7.2 0.0 all-gather.2.cloned.1.call-start
  7.3 0.8 convert_element_type.43
  8.1 1.2 %fusion.9 = f32[64]{0:T(128)S(1)} fusion(bf16[1,64,4096]{2,1,0:T(8,128)(2,1)} %param.8), kind=kLoop, calls=%fused_computation.15 | loop fusion | flops 786368 | bytes 524544 | tf_op jit(solution)/shard_map/reduce_sum | solution.py:33
  9.4 2.0 %fusion.11 = bf16[64,4096]{1,0:T(8,128)(2,1)} fusion(bf16[1,64,4096]{2,1,0:T(8,128)(2,1)} %param.8, f32[4096]{0:T(1024)S(1)} %convert_element_type.43, f32[64]{0:T(128)S(1)} %add_rsqrt_fusion), kind=kLoop, calls=%fused_computation.17 | loop fusion | flops 1048576 | bytes 1065216 | tf_op jit(solution)/shard_map/convert_element_type | solution.py:35
  11.4 0.0 all-gather.2.cloned.1.call-update
  11.4 0.0 reduce-scatter.2.cloned.1.call-start
  11.5 0.0 copy-done.1
  11.5 0.0 copy-done.2
  11.6 0.5 fusion.24
  12.1 24.8 %all-gather.2.cloned.1.call-done = bf16[256,4096]{1,0:T(8,128)(2,1)} async-done(((bf16[64,4096]{1,0:T(8,128)(2,1)}), bf16[256,4096]{1,0:T(8,128)(2,1)}) %all-gather.2.cloned.1.call-update) | async-done | bytes 2097168 | tf_op jit(solution)/shard_map/all_gather | solution.py:44
  36.9 0.0 copy-done.3
  36.9 7.5 %fusion.5 = f32[256,1280]{1,0:T(8,128)S(1)} fusion(bf16[256,4096]{1,0:T(8,128)(2,1)} %all-gather.2.cloned.1.call-done, bf16[4096,256]{1,0:T(8,128)(2,1)S(1)} %copy-done.3, bf16[4096,1024]{1,0:T(8,128)(2,1)} %param.10, f32[1280]{0:T(1024)S(1)} %maximum_convert_fusion), kind=kOutput, calls=%fused_computation.6 | convolution fusion | flops 2705653760 | bytes 13898752 | tf_op jit(solution)/shard_map/dot_general | solution.py:43
  44.4 0.1 slice_bitcast_fusion
  44.5 7.2 %all_gather.7 = bf16[256,1024]{1,0:T(8,128)(2,1)S(1)} all-gather(bf16[256,256]{1,0:T(8,128)(2,1)S(1)} %slice.37), channel_id=1, replica_groups=mesh['dp'=8,'tensor'=4] {'tensor'}, dimensions={1}, use_global_device_ids=true | all-gather | bytes 655360 | tf_op jit(solution)/shard_map/all_gather | solution.py:53
  51.7 0.5 subtract_convert_fusion.1
  52.3 0.2 copy.19
  52.5 0.3 fusion.39
  52.8 0.4 subtract_convert_fusion
  53.2 2.4 %fusion.40 = (f32[8,256]{1,0:T(8,128)S(1)}, f32[8,256,256]{1,2,0:T(8,128)}) fusion(pred[256,256]{0,1:T(8,128)(4,1)S(1)} %iota_compare_fusion, bf16[256,8,64]{2,0,1:T(8,128)(2,1)S(1)} %get-tuple-element.3, bf16[256,8,64]{2,0,1:T(8,128)(2,1)S(1)} %get-tuple-element.2, bf16[256,1,64]{2,0,1:T(8,128)(2,1)S(1)} %get-tuple-element.7, ...), kind=kOutput, calls=%fused_computation.54 | convolution fusion | flops 137494784 | bytes 2760704 | tf_op jit(solution)/shard_map/sub | solution.py:70
  55.6 1.9 %convolution_convert_fusion.1 = bf16[128,8,256]{2,0,1:T(8,128)(2,1)S(1)} fusion(f32[8,256,256]{1,2,0:T(8,128)} %get-tuple-element.11, f32[8,256]{1,0:T(8,128)S(1)} %get-tuple-element.10, bf16[256,1024]{1,0:T(8,128)(2,1)S(1)} %all_gather.7, s32[]{:T(128)S(6)} %select_n.16), kind=kOutput, calls=%fused_computation.13 | convolution fusion | flops 135528448 | bytes 2695172 | tf_op jit(solution)/shard_map/hqk,kd->qhd/dot_general | solution.py:71
  57.5 7.1 %convolution_convert_fusion = bf16[256,4096]{1,0:T(8,128)(2,1)} fusion(bf16[256,1024]{0,1:T(8,128)(2,1)S(1)} %bitcast.49, bf16[1024,4096]{1,0:T(8,128)(2,1)} %param.14), kind=kOutput, calls=%fused_computation.5 | convolution fusion | flops 2148532224 | bytes 11010048 | tf_op jit(solution)/shard_map/dot_general | solution.py:77
  64.6 0.0 reduce-scatter.2.cloned.1.call-update
  64.7 0.0 copy-done
  64.7 0.5 convolution_bitcast_fusion
  65.2 5.7 %fusion.43 = f32[1,4096]{1,0:T(1,128)S(1)} fusion(f32[1024,1]{0,1:T(1,128)S(1)} %convolution_bitcast_fusion, bf16[1024,4096]{1,0:T(8,128)(2,1)} %param.14), kind=kOutput, calls=%fused_computation.55 | convolution fusion | flops 50331648 | bytes 8409088 | tf_op jit(solution)/shard_map/dot_general | solution.py:86
  70.9 39.7 %psum.7 = f32[4096]{0:T(1024)S(1)} all-reduce(f32[4096]{0:T(1024)S(1)} %bitcast.51), channel_id=1, replica_groups=mesh['dp'=8,'tensor'=4] {'dp','tensor'}, use_global_device_ids=true, to_apply=%region_4.5 | all-reduce | flops 4096 | bytes 32768 | tf_op jit(solution)/shard_map/psum | solution.py:87
  110.6 0.6 broadcast_multiply_fusion
  111.2 0.0 reduce-scatter.2.cloned.1.call-done
  (6 shorter events, 0.1 us)
Async XLA Ops:
  7.2 57.5 %copy-start = (f32[1,256]{1,0:T(1,128)S(1)}, f32[1,256]{1,0:T(1,128)}, u32[]{:S(2)}) copy-start(f32[1,256]{1,0:T(1,128)} %param.15) | copy-start | bytes 3076
  7.2 4.3 %copy-start.1 = (bf16[1024]{0:T(1024)(128)(2,1)S(1)}, bf16[1024]{0:T(1024)(128)(2,1)}, u32[]{:S(2)}) copy-start(bf16[1024]{0:T(1024)(128)(2,1)} %param.11) | copy-start | bytes 6148
  7.2 4.3 %copy-start.2 = (bf16[256]{0:T(256)(128)(2,1)S(1)}, bf16[256]{0:T(256)(128)(2,1)}, u32[]{:S(2)}) copy-start(bf16[256]{0:T(256)(128)(2,1)} %param.13) | copy-start | bytes 1540
  7.2 29.7 %copy-start.3 = (bf16[4096,256]{1,0:T(8,128)(2,1)S(1)}, bf16[4096,256]{1,0:T(8,128)(2,1)}, u32[]{:S(2)}) copy-start(bf16[4096,256]{1,0:T(8,128)(2,1)} %param.12) | copy-start | bytes 6291460
  7.2 29.7 %all-gather.2.cloned.1.call-start = ((), (), s32[]{:S(2)}) async-start(), calls=%async_computation.1 | async-start | bytes 2621440 | tf_op jit(solution)/shard_map/all_gather | solution.py:44
  11.4 99.8 %reduce-scatter.2.cloned.1.call-start = ((), (), s32[]{:S(2)}) async-start(), calls=%async_computation.2 | async-start | bytes 2621440 | tf_op jit(solution)/shard_map/reduce_scatter | solution.py:76
Sparse Core Ops, SparseCore 0:
  11.5 25.2 all-gather.1
  64.8 31.3 reduce-scatter.1
where the time goes:
time: 118 us
  blocking collectives  46.9 us (40%)
  matrix products  25.1 us (21%)
  waiting for transfers between devices  24.8 us (21%)
  between operations  14.2 us (12%)
  other arithmetic  6.25 us (5%)
    psum x1, blocking collectives, local(): total = lax.psum(term, ('dp', 'tensor'))  39.7 us
    all_gather x1, waiting for transfers between devices, local(): lax.all_gather(normed, 'tensor', axis=0, tiled=True)  24.8 us
    dot_general x1, matrix products, local(): jnp.dot(lax.all_gather(normed, 'tensor', axis=0, tiled=True), joined_w, p...  7.53 us
    all_gather x1, blocking collectives, local(): kv_whole = lax.all_gather(kv_local, 'tensor', axis=1, tiled=True)  7.16 us
    dot_general x1, matrix products, local(): jnp.dot(context, wo, preferred_element_type=jnp.float32)  7.11 us
    dot_general x1, matrix products, local(): jnp.dot(summary, wo.astype(jnp.float32), precision=lax.Precision.HIGHEST)  5.68 us
  transfers between devices with their start and end apart: 2, of which 1 were waited for; matrix products, arithmetic and copies ran while one was open for 6% of the time, Pallas kernels for 0%

commit v1 on v0

--- a/solution.py
+++ b/solution.py
@@ -1,3 +1,4 @@
+import functools
 import jax
 import jax.numpy as jnp
 from jax import lax
@@ -8,6 +9,13 @@
 HD = 128
 EPS = 1e-06
 THETA = 1000000.0
+
+
+def connect_packet(incoming_x, chip_axis, across):
+    return lax.psum(lax.psum(incoming_x, axis_name=across), axis_name=chip_axis)
+
+
+touch_the_sites = functools.partial(connect_packet, chip_axis="dp", across="tensor")
 
 
 def rope(values, head_size):
@@ -84,7 +92,7 @@
         check_weights[0], context.astype(jnp.float32), precision=lax.Precision.HIGHEST
     )
     term = jnp.dot(summary, wo.astype(jnp.float32), precision=lax.Precision.HIGHEST)
-    total = lax.psum(term, ("dp", "tensor"))
+    total = touch_the_sites(term)
     checksum = total / jnp.sqrt(jnp.float32(seq_rows * lax.axis_size("dp")))
     return (attended, checksum)
 

time: 118 us -> 126 us (1.068)
  blocking collectives: 46.9 us -> 54.7 us
    psum x1 -> x2, blocking collectives: 39.7 us -> 47.5 us  [connect_packet(): return lax.psum(lax.psum(incoming_x, axis_name=across), axis_name=chip_axis)]
where the time goes in v1:
time: 126 us
  blocking collectives  54.7 us (43%)
  matrix products  25.1 us (20%)
  waiting for transfers between devices  24.8 us (20%)
  between operations  14.2 us (11%)
  other arithmetic  6.25 us (5%)
    psum x2, blocking collectives, connect_packet(): return lax.psum(lax.psum(incoming_x, axis_name=across), axis_name=chip_axis)  47.5 us
    all_gather x1, waiting for transfers between devices, local(): lax.all_gather(normed, 'tensor', axis=0, tiled=True)  24.8 us
    dot_general x1, matrix products, local(): jnp.dot(lax.all_gather(normed, 'tensor', axis=0, tiled=True), joined_w, p...  7.53 us
    all_gather x1, blocking collectives, local(): kv_whole = lax.all_gather(kv_local, 'tensor', axis=1, tiled=True)  7.16 us
    dot_general x1, matrix products, local(): jnp.dot(context, wo, preferred_element_type=jnp.float32)  7.12 us
    dot_general x1, matrix products, local(): jnp.dot(summary, wo.astype(jnp.float32), precision=lax.Precision.HIGHEST)  5.68 us
  transfers between devices with their start and end apart: 2, of which 1 were waited for; matrix products, arithmetic and copies ran while one was open for 6% of the time, Pallas kernels for 0%

profile of v1, /device:TPU:0, one launch (start us, length us, event | category | flops | bytes accessed | tf_op | source)
XLA Modules:
  0.0 125.9 jit_solution(10651515179446965862)
XLA Ops:
  7.2 0.0 copy-start
  7.2 0.0 copy-start.1
  7.2 0.0 copy-start.2
  7.2 0.0 copy-start.3
  7.2 0.0 all-gather.2.cloned.1.call-start
  7.3 0.8 convert_element_type.43
  8.1 1.2 fusion.9
  9.4 2.0 %fusion.11 = bf16[64,4096]{1,0:T(8,128)(2,1)} fusion(bf16[1,64,4096]{2,1,0:T(8,128)(2,1)} %param.8, f32[4096]{0:T(1024)S(1)} %convert_element_type.43, f32[64]{0:T(128)S(1)} %add_rsqrt_fusion), kind=kLoop, calls=%fused_computation.17 | loop fusion | flops 1048576 | bytes 1065216 | tf_op jit(solution)/shard_map/convert_element_type | solution.py:43
  11.4 0.0 all-gather.2.cloned.1.call-update
  11.4 0.0 reduce-scatter.2.cloned.1.call-start
  11.5 0.0 copy-done.1
  11.5 0.0 copy-done.2
  11.6 0.5 fusion.24
  12.1 24.8 %all-gather.2.cloned.1.call-done = bf16[256,4096]{1,0:T(8,128)(2,1)} async-done(((bf16[64,4096]{1,0:T(8,128)(2,1)}), bf16[256,4096]{1,0:T(8,128)(2,1)}) %all-gather.2.cloned.1.call-update) | async-done | bytes 2097168 | tf_op jit(solution)/shard_map/all_gather | solution.py:52
  36.9 0.0 copy-done.3
  36.9 7.5 %fusion.5 = f32[256,1280]{1,0:T(8,128)S(1)} fusion(bf16[256,4096]{1,0:T(8,128)(2,1)} %all-gather.2.cloned.1.call-done, bf16[4096,256]{1,0:T(8,128)(2,1)S(1)} %copy-done.3, bf16[4096,1024]{1,0:T(8,128)(2,1)} %param.10, f32[1280]{0:T(1024)S(1)} %maximum_convert_fusion), kind=kOutput, calls=%fused_computation.6 | convolution fusion | flops 2705653760 | bytes 13898752 | tf_op jit(solution)/shard_map/dot_general | solution.py:51
  44.4 0.1 slice_bitcast_fusion
  44.5 7.2 %all_gather.7 = bf16[256,1024]{1,0:T(8,128)(2,1)S(1)} all-gather(bf16[256,256]{1,0:T(8,128)(2,1)S(1)} %slice.37), channel_id=1, replica_groups=mesh['dp'=8,'tensor'=4] {'tensor'}, dimensions={1}, use_global_device_ids=true | all-gather | bytes 655360 | tf_op jit(solution)/shard_map/all_gather | solution.py:61
  51.7 0.5 subtract_convert_fusion.1
  52.3 0.2 copy.19
  52.5 0.3 fusion.39
  52.8 0.4 subtract_convert_fusion
  53.2 2.4 %fusion.40 = (f32[8,256]{1,0:T(8,128)S(1)}, f32[8,256,256]{1,2,0:T(8,128)}) fusion(pred[256,256]{0,1:T(8,128)(4,1)S(1)} %iota_compare_fusion, bf16[256,8,64]{2,0,1:T(8,128)(2,1)S(1)} %get-tuple-element.3, bf16[256,8,64]{2,0,1:T(8,128)(2,1)S(1)} %get-tuple-element.2, bf16[256,1,64]{2,0,1:T(8,128)(2,1)S(1)} %get-tuple-element.7, ...), kind=kOutput, calls=%fused_computation.54 | convolution fusion | flops 137494784 | bytes 2760704 | tf_op jit(solution)/shard_map/sub | solution.py:78
  55.6 1.9 %convolution_convert_fusion.1 = bf16[128,8,256]{2,0,1:T(8,128)(2,1)S(1)} fusion(f32[8,256,256]{1,2,0:T(8,128)} %get-tuple-element.11, f32[8,256]{1,0:T(8,128)S(1)} %get-tuple-element.10, bf16[256,1024]{1,0:T(8,128)(2,1)S(1)} %all_gather.7, s32[]{:T(128)S(6)} %select_n.16), kind=kOutput, calls=%fused_computation.13 | convolution fusion | flops 135528448 | bytes 2695172 | tf_op jit(solution)/shard_map/hqk,kd->qhd/dot_general | solution.py:79
  57.5 7.1 %convolution_convert_fusion = bf16[256,4096]{1,0:T(8,128)(2,1)} fusion(bf16[256,1024]{0,1:T(8,128)(2,1)S(1)} %bitcast.49, bf16[1024,4096]{1,0:T(8,128)(2,1)} %param.14), kind=kOutput, calls=%fused_computation.5 | convolution fusion | flops 2148532224 | bytes 11010048 | tf_op jit(solution)/shard_map/dot_general | solution.py:85
  64.6 0.0 reduce-scatter.2.cloned.1.call-update
  64.7 0.0 copy-done
  64.7 0.5 convolution_bitcast_fusion
  65.2 5.7 %fusion.43 = f32[1,4096]{1,0:T(1,128)S(1)} fusion(f32[1024,1]{0,1:T(1,128)S(1)} %convolution_bitcast_fusion, bf16[1024,4096]{1,0:T(8,128)(2,1)} %param.14), kind=kOutput, calls=%fused_computation.55 | convolution fusion | flops 50331648 | bytes 8409088 | tf_op jit(solution)/shard_map/dot_general | solution.py:94
  70.9 10.5 %psum.14 = f32[4096]{0:T(1024)S(1)} all-reduce(f32[4096]{0:T(1024)S(1)} %bitcast.51), channel_id=1, replica_groups=mesh['dp'=8,'tensor'=4] {'tensor'}, use_global_device_ids=true, to_apply=%region_4.5 | all-reduce | flops 4096 | bytes 32768 | tf_op jit(solution)/shard_map/psum | solution.py:15
  81.3 37.1 %psum.15 = f32[4096]{0:T(1024)S(1)} all-reduce(f32[4096]{0:T(1024)S(1)} %psum.14), channel_id=1, replica_groups=mesh['dp'=8,'tensor'=4] {'dp'}, use_global_device_ids=true, to_apply=%region_5.6 | all-reduce | flops 4096 | bytes 32768 | tf_op jit(solution)/shard_map/psum | solution.py:15
  118.4 0.6 broadcast_multiply_fusion
  (7 shorter events, 0.1 us)
Async XLA Ops:
  7.2 57.5 %copy-start = (f32[1,256]{1,0:T(1,128)S(1)}, f32[1,256]{1,0:T(1,128)}, u32[]{:S(2)}) copy-start(f32[1,256]{1,0:T(1,128)} %param.15) | copy-start | bytes 3076
  7.2 4.3 %copy-start.1 = (bf16[1024]{0:T(1024)(128)(2,1)S(1)}, bf16[1024]{0:T(1024)(128)(2,1)}, u32[]{:S(2)}) copy-start(bf16[1024]{0:T(1024)(128)(2,1)} %param.11) | copy-start | bytes 6148
  7.2 4.3 %copy-start.2 = (bf16[256]{0:T(256)(128)(2,1)S(1)}, bf16[256]{0:T(256)(128)(2,1)}, u32[]{:S(2)}) copy-start(bf16[256]{0:T(256)(128)(2,1)} %param.13) | copy-start | bytes 1540
  7.2 29.7 %copy-start.3 = (bf16[4096,256]{1,0:T(8,128)(2,1)S(1)}, bf16[4096,256]{1,0:T(8,128)(2,1)}, u32[]{:S(2)}) copy-start(bf16[4096,256]{1,0:T(8,128)(2,1)} %param.12) | copy-start | bytes 6291460
  7.2 29.7 %all-gather.2.cloned.1.call-start = ((), (), s32[]{:S(2)}) async-start(), calls=%async_computation.1 | async-start | bytes 2621440 | tf_op jit(solution)/shard_map/all_gather | solution.py:52
  11.4 107.6 %reduce-scatter.2.cloned.1.call-start = ((), (), s32[]{:S(2)}) async-start(), calls=%async_computation.2 | async-start | bytes 2621440 | tf_op jit(solution)/shard_map/reduce_scatter | solution.py:84
Sparse Core Ops, SparseCore 0:
  11.5 25.2 all-gather.1
  64.8 31.1 reduce-scatter.1
